TPU v7x, 32 devices: a whole 2x2x4 slice. The times are simulated.
32 devices in a mesh: rows: 8 (over y, x, core), cols: 4 (over z).
Axes of the slice: x: 2, y: 2, z: 4, core: 2. Of those that a mesh axis runs over, the one named last changes fastest.
Arguments:
- token_ids: int32 [16, 2048], P('rows', 'cols'), may hold values from 0 to 131071, as said below
- lengths: int32 [16], P('rows'), may hold values from 1 to 2048
- table: bfloat16 [131072, 512], P('rows', 'cols'), may hold values from -6 to 6
- attn_gain: float32 [512], replicated, may hold values from 0.1 to 1.9
- w_qkv: bfloat16 [512, 1536], replicated, may hold values from -2 to 2
- w_out: bfloat16 [512, 512], replicated, may hold values from -0.25 to 0.25
- mlp_gain: float32 [512], replicated, may hold values from 0.1 to 1.9
- w_in: bfloat16 [512, 4096], replicated, may hold values from -0.25 to 0.25
- w_down: bfloat16 [2048, 512], replicated, may hold values from -0.125 to 0.125
Outputs:
- layer_out: bfloat16 [16, 2048, 512], P('rows', 'cols')
Inputs may be any that keep to these rules, and one draw needn't show every extreme that they name: `token_ids`: ids lie in 0 to 131071. In each aligned block of 2 histories (4096 positions) at most 1365 ids fall in any one block of 16384 consecutive table rows, and in every such block of histories some block of table rows receives exactly 1365.
All inputs are finite; a program needn't handle non-finite values.
Results may differ from a plain program's by a relative error of at most 0.012.
Values may be sent and summed in bfloat16 or wider, within the bound.
A program may use at most 192 MiB of HBM per device.

v0:
```python
import jax
import jax.numpy as jnp
from jax import lax
from jax.sharding import PartitionSpec as P

D = 512
HEADS = 8
FF = 2048


def rms_norm(values_f32, gain):
    mean_sq = jnp.mean(values_f32 * values_f32, axis=-1, keepdims=True)
    return values_f32 * lax.rsqrt(mean_sq + 1e-06) * gain


def local(token_ids, lengths, table, attn_gain, w_qkv, w_out, mlp_gain, w_in, w_down):
    batch_dev, quarter = token_ids.shape
    col_count = lax.axis_size("cols")
    row_count = lax.axis_size("rows")
    full_len = quarter * col_count
    block_rows, col_width = table.shape
    zero_bf = jnp.zeros((), jnp.bfloat16)
    own_ids = lax.all_gather(token_ids, "cols", axis=1, tiled=True)
    flat_ids = own_ids.reshape(-1)
    token_count = flat_ids.shape[0]
    capacity = 8 * token_count // (3 * row_count)
    owner_block = flat_ids // block_rows
    onehot = (owner_block[:, None] == jnp.arange(row_count, dtype=jnp.int32)[None, :]).astype(
        jnp.int32
    )
    slot_rank = jnp.sum((jnp.cumsum(onehot, axis=0) - 1) * onehot, axis=1)
    slot_index = owner_block * capacity + slot_rank
    requests = jnp.full((row_count * capacity,), -1, jnp.int32)
    requests = (
        requests.at[slot_index]
        .set(flat_ids - owner_block * block_rows)
        .reshape(row_count, capacity)
    )
    asked = lax.all_to_all(requests, "rows", split_axis=0, concat_axis=0, tiled=True)
    looked = jnp.take(table, jnp.maximum(asked, 0), axis=0)
    looked = jnp.where((asked >= 0)[..., None], looked, zero_bf)
    returned = lax.all_to_all(looked, "rows", split_axis=0, concat_axis=0, tiled=True)
    embedded = returned.reshape(row_count * capacity, col_width)[slot_index]
    embedded = embedded.reshape(batch_dev, full_len, col_width)
    sequence = lax.all_to_all(embedded, "cols", split_axis=1, concat_axis=2, tiled=True)
    residual = sequence.astype(jnp.float32)
    normed = rms_norm(residual, attn_gain).astype(jnp.bfloat16)
    projected = jnp.einsum("bqe,ef->bqf", normed, w_qkv, preferred_element_type=jnp.float32).astype(
        jnp.bfloat16
    )
    head_dim = D // HEADS
    queries = projected[..., :D].reshape(batch_dev, quarter, HEADS, head_dim)
    keys = projected[..., D : 2 * D]
    values = projected[..., 2 * D :]
    query_pos = lax.axis_index("cols") * quarter + jnp.arange(quarter, dtype=jnp.int32)
    running_max = jnp.full((batch_dev, HEADS, quarter), -1e30, jnp.float32)
    key_piece = lax.all_gather(keys, "cols", axis=1, tiled=True)
    value_piece = lax.all_gather(values, "cols", axis=1, tiled=True)
    piece_len = key_piece.shape[1]
    key_heads = key_piece.reshape(batch_dev, piece_len, HEADS, head_dim)
    value_heads = value_piece.reshape(batch_dev, piece_len, HEADS, head_dim)
    scores = (
        jnp.einsum("bqhd,bkhd->bhqk", queries, key_heads, preferred_element_type=jnp.float32)
        * 0.125
    )
    key_pos = jnp.arange(piece_len, dtype=jnp.int32)
    causal = key_pos[None, :] <= query_pos[:, None]
    inside = key_pos[None, :] < lengths[:, None]
    valid = causal[None, None, :, :] & inside[:, None, None, :]
    scores = jnp.where(valid, scores, -1e30)
    new_max = jnp.maximum(running_max, jnp.max(scores, axis=-1))
    probs = jnp.where(valid, jnp.exp(scores - new_max[..., None]), 0.0)
    running_sum = jnp.sum(probs, axis=-1)
    weighted = jnp.einsum(
        "bhqk,bkhd->bhqd",
        probs.astype(jnp.bfloat16),
        value_heads,
        preferred_element_type=jnp.float32,
    )
    final_max, final_sum, weighted = (new_max, running_sum, weighted)
    summed = weighted / final_sum[..., None]
    attended = (
        jnp.transpose(summed, (0, 2, 1, 3)).reshape(batch_dev, quarter, D).astype(jnp.bfloat16)
    )
    hidden = (
        residual + jnp.einsum("bqe,ef->bqf", attended, w_out, preferred_element_type=jnp.float32)
    ).astype(jnp.bfloat16)
    hidden_f32 = hidden.astype(jnp.float32)
    normed_two = rms_norm(hidden_f32, mlp_gain).astype(jnp.bfloat16)
    gate_up = jnp.einsum("bqe,ef->bqf", normed_two, w_in, preferred_element_type=jnp.float32)
    act = (jax.nn.silu(gate_up[..., :FF]) * gate_up[..., FF:]).astype(jnp.bfloat16)
    return (
        hidden_f32 + jnp.einsum("bqf,fe->bqe", act, w_down, preferred_element_type=jnp.float32)
    ).astype(jnp.bfloat16)


def solution(mesh):
    in_specs = (P("rows", "cols"), P("rows"), P("rows", "cols"), P(), P(), P(), P(), P(), P())
    out_specs = P("rows", "cols", None)
    return jax.shard_map(local, mesh=mesh, in_specs=in_specs, out_specs=out_specs, check_vma=False)
```

profile of v0, /device:TPU:26, one launch (start us, length us, event | category | flops | bytes accessed | tf_op | source)
XLA Modules:
  0.0 410.2 jit_solution(13161058633130101524)
XLA Ops:
  6.5 13.5 %all_gather.9 = s32[2,2048]{1,0:T(2,128)S(1)} all-gather(s32[2,512]{1,0:T(2,128)} %param.9), channel_id=1, replica_groups=mesh['rows'=8,'cols'=4] {'cols'}, dimensions={1}, use_global_device_ids=true | all-gather | bytes 20480 | tf_op jit(solution)/shard_map/all_gather | solution.py:23
  20.1 2.3 reduce-window.6
  22.4 0.3 slice_reduce_fusion
  22.7 0.2 reduce-window.9
  22.9 0.1 add_bitcast_fusion
  23.1 0.1 fusion.32
  23.2 0.1 compare_select_fusion
  23.3 15.5 %scatter_custom_fusion = s32[10920]{0:T(1024)S(1)} fusion(s32[4096]{0:T(1024)S(1)} %bitcast.81, s32[4096]{0:T(1024)S(1)} %get-tuple-element.10, s32[]{:T(128)} %constant.27.clone.1), kind=kCustom, calls=%fused_computation.65 | custom fusion | bytes 43684 | tf_op jit(solution)/shard_map/scatter | solution.py:36
  38.8 0.1 all_to_all.16
  38.9 7.5 %all_to_all.23 = s32[8,1,1365]{2,1,0:T(1,128)S(1)} all-to-all(s32[8,1,1365]{2,1,0:T(1,128)S(1)} %all_to_all.16), channel_id=1, replica_groups=mesh['rows'=8,'cols'=4] {'rows'}, dimensions={0} | all-to-all | bytes 87360 | tf_op jit(solution)/shard_map/all_to_all | solution.py:39
  46.5 0.1 reshape.265
  46.6 23.7 %gather_fusion = bf16[10920,128]{1,0:T(8,128)(2,1)} fusion(bf16[16384,128]{1,0:T(8,128)(2,1)} %param.11, s32[11264]{0:T(1024)S(1)} %pad_clamp_fusion), kind=kCustom, calls=%fused_computation | custom fusion | bytes 5634720 | tf_op jit(solution)/shard_map/jit(_take)/gather | solution.py:40
  70.3 4.2 %reshape.264 = bf16[8,1365,128]{2,1,0:T(8,128)(2,1)} reshape(bf16[10920,128]{1,0:T(8,128)(2,1)} %gather_fusion) | data formatting | bytes 5591040 | tf_op jit(solution)/shard_map/jit(_take)/gather | solution.py:40
  74.5 10.2 %select_select_fusion = bf16[8,1365,128]{2,1,0:T(8,128)(2,1)} fusion(bf16[8,1365,128]{2,1,0:T(8,128)(2,1)} %reshape.264, pred[8,1365]{1,0:T(8,128)(4,1)S(1)} %get-tuple-element.9, pred[8,1365]{1,0:T(8,128)(4,1)S(1)} %get-tuple-element.8), kind=kLoop, calls=%fused_computation.21 | loop fusion | flops 2795520 | bytes 5612880 | tf_op jit(solution)/shard_map/jit(_where)/select_n | solution.py:41
  84.7 5.8 %all-to-all-start.1 = ((bf16[8,1365,128]{2,1,0:T(8,128)(2,1)}), bf16[8,1365,128]{2,1,0:T(8,128)(2,1)}, u32[]{:S(2)}, u32[]{:S(2)}) async-start(bf16[8,1365,128]{2,1,0:T(8,128)(2,1)} %select_select_fusion), calls=%async_computation.1 | async-start | bytes 5603328 | tf_op jit(solution)/shard_map/all_to_all | solution.py:42
  90.4 32.8 %all-to-all-done.1 = bf16[8,1365,128]{2,1,0:T(8,128)(2,1)} async-done(((bf16[8,1365,128]{2,1,0:T(8,128)(2,1)}), bf16[8,1365,128]{2,1,0:T(8,128)(2,1)}, u32[]{:S(2)}, u32[]{:S(2)}) %all-to-all-start.1) | async-done | bytes 2795552 | tf_op jit(solution)/shard_map/all_to_all | solution.py:42
  123.2 4.2 %reshape.256 = bf16[10920,128]{1,0:T(8,128)(2,1)} reshape(bf16[8,1365,128]{2,1,0:T(8,128)(2,1)} %all-to-all-done.1) | data formatting | bytes 5591040 | tf_op jit(solution)/shard_map/reshape | solution.py:43
  127.4 13.2 %gather_fusion.1 = bf16[4096,128]{1,0:T(8,128)(2,1)S(1)} fusion(bf16[10920,128]{1,0:T(8,128)(2,1)} %reshape.256, s32[4096]{0:T(1024)S(1)} %broadcast_clamp_fusion), kind=kCustom, calls=%fused_computation.1 | custom fusion | bytes 2113536 | tf_op jit(solution)/shard_map/gather | solution.py:43
  140.6 8.7 %copy.57 = bf16[2,2048,128]{2,0,1:T(2,128)(2,1)S(1)} copy(bf16[2,2048,128]{2,1,0:T(8,128)(2,1)S(1)} %bitcast.75) | data formatting | bytes 2097152 | tf_op jit(solution)/shard_map/reshape | solution.py:44
  149.3 28.5 %all_to_all.24 = bf16[2,2048,128]{2,0,1:T(2,128)(2,1)S(1)} all-to-all(bf16[2,2048,128]{2,0,1:T(2,128)(2,1)S(1)} %copy.57), channel_id=1, replica_groups=mesh['rows'=8,'cols'=4] {'cols'}, dimensions={1} | all-to-all | bytes 2097152 | tf_op jit(solution)/shard_map/all_to_all | solution.py:45
  177.8 1.5 copy_convert_fusion
  179.3 2.9 copy.59
  182.2 0.6 multiply_reduce_fusion
  182.9 1.8 fusion.18
  184.7 3.2 convolution_convert_fusion
  188.0 0.0 copy-start.3
  188.0 1.7 fusion.44
  189.7 0.0 all-gather.3.cloned.1.call-update
  189.7 0.0 all-gather.5.cloned.1.call-start
  189.8 0.1 iota_compare_fusion.3
  189.9 0.7 iota_compare_fusion
  190.5 2.6 broadcast_and_fusion
  193.2 1.3 copy.61
  194.5 0.0 all-gather.5.cloned.1.call-update
  194.5 73.6 %all-gather.3.cloned.1.call-done = bf16[2,2048,512]{2,1,0:T(8,128)(2,1)} async-done(((bf16[2,512,512]{2,1,0:T(8,128)(2,1)}), bf16[2,2048,512]{2,1,0:T(8,128)(2,1)}) %all-gather.3.cloned.1.call-update) | async-done | bytes 4194320 | tf_op jit(solution)/shard_map/all_gather | solution.py:57
  268.0 6.3 %copy.62 = bf16[2,2048,512]{1,2,0:T(8,128)(2,1)} copy(bf16[2,2048,512]{2,1,0:T(8,128)(2,1)} %all-gather.3.cloned.1.call-done) | data formatting | bytes 8388608 | tf_op jit(solution)/shard_map/all_gather | solution.py:57
  274.3 27.4 %fusion = (f32[2,8,512]{2,1,0:T(8,128)S(1)}, f32[2,8,512,2048]{3,2,1,0:T(8,128)}) fusion(pred[2,512,2048]{2,1,0:T(8,128)(4,1)} %broadcast_and_fusion, bf16[2,512,8,64]{1,3,2,0:T(8,128)(2,1)} %bitcast.74, bf16[2,2048,8,64]{1,3,2,0:T(8,128)(2,1)} %bitcast.72), kind=kOutput, calls=%fused_computation.5 | convolution fusion | flops 2197807104 | bytes 74481664 | tf_op jit(solution)/shard_map/bqhd,bkhd->bhqk/dot_general | solution.py:63
  301.7 22.4 %fusion.1 = f32[2,8,512]{2,1,0:T(8,128)S(1)} fusion(f32[2,8,512,2048]{3,2,1,0:T(8,128)} %get-tuple-element.13, f32[2,8,512]{2,1,0:T(8,128)S(1)} %broadcast_maximum_fusion, pred[2,512,2048]{2,1,0:T(8,128)(4,1)S(1)} %copy-done.1), kind=kLoop, calls=%fused_computation.6 | loop fusion | flops 83877888 | bytes 69271552 | tf_op jit(solution)/shard_map/reduce_sum | solution.py:73
  324.1 24.8 %all-gather.5.cloned.1.call-done = bf16[2,2048,512]{2,1,0:T(8,128)(2,1)} async-done(((bf16[2,512,512]{2,1,0:T(8,128)(2,1)}), bf16[2,2048,512]{2,1,0:T(8,128)(2,1)}) %all-gather.5.cloned.1.call-update) | async-done | bytes 4194320 | tf_op jit(solution)/shard_map/all_gather | solution.py:58
  348.9 6.3 %copy.63 = bf16[2,2048,512]{1,2,0:T(8,128)(2,1)} copy(bf16[2,2048,512]{2,1,0:T(8,128)(2,1)} %all-gather.5.cloned.1.call-done) | data formatting | bytes 8388608 | tf_op jit(solution)/shard_map/all_gather | solution.py:58
  355.2 27.0 %fusion.16 = bf16[2,512,8,64]{1,3,2,0:T(8,128)(2,1)S(1)} fusion(bf16[2,2048,8,64]{1,3,2,0:T(8,128)(2,1)} %bitcast.76, f32[2,8,512,2048]{3,2,1,0:T(8,128)} %get-tuple-element.13, f32[2,8,512]{2,1,0:T(8,128)S(1)} %broadcast_maximum_fusion, pred[2,512,2048]{2,1,0:T(8,128)(4,1)} %broadcast_and_fusion, f32[2,512,8]{1,2,0:T(8,128)S(1)} %bitcast.85), kind=kOutput, calls=%fused_computation.28 | convolution fusion | flops 2232418304 | bytes 74514432 | tf_op jit(solution)/shard_map/bhqk,bkhd->bhqd/dot_general | solution.py:74
  382.1 0.0 copy-start.4
  382.2 0.0 copy-start.5
  382.2 2.7 fusion.11
  384.9 0.3 copy-done.4
  385.1 8.3 %fusion.7 = f32[2,512,4096]{2,1,0:T(8,128)} fusion(bf16[512,4096]{1,0:T(8,128)(2,1)S(1)} %copy-done.4, bf16[2,512,512]{1,2,0:T(8,128)(2,1)S(1)} %get-tuple-element.15, f32[512]{0:T(512)S(1)} %copy-done.5, f32[2,512]{1,0:T(2,128)S(1)} %add_rsqrt_fusion), kind=kOutput, calls=%fused_computation.12 | convolution fusion | flops 4297064448 | bytes 22026240 | tf_op jit(solution)/shard_map/bqe,ef->bqf/dot_general | solution.py:90
  393.5 8.6 %fusion.14 = bf16[2,512,512]{1,2,0:T(8,128)(2,1)S(1)} fusion(bf16[2,512,512]{1,2,0:T(8,128)(2,1)S(1)} %get-tuple-element.15, bf16[2048,512]{1,0:T(8,128)(2,1)S(1)} %copy-done, f32[2,512,4096]{2,1,0:T(8,128)} %fusion.7), kind=kOutput, calls=%fused_computation.25 | convolution fusion | flops 2161639424 | bytes 20971520 | tf_op jit(solution)/shard_map/bqf,fe->bqe/dot_general | solution.py:93
  402.0 1.3 copy.68
  (25 shorter events, 0.2 us)
Async XLA Ops:
  6.5 386.9 %copy-start = (bf16[2048,512]{1,0:T(8,128)(2,1)S(1)}, bf16[2048,512]{1,0:T(8,128)(2,1)}, u32[]{:S(2)}) copy-start(bf16[2048,512]{1,0:T(8,128)(2,1)} %param.17) | copy-start | bytes 6291460
  84.7 38.5 %all-to-all-start.1 = ((bf16[8,1365,128]{2,1,0:T(8,128)(2,1)}), bf16[8,1365,128]{2,1,0:T(8,128)(2,1)}, u32[]{:S(2)}, u32[]{:S(2)}) async-start(bf16[8,1365,128]{2,1,0:T(8,128)(2,1)} %select_select_fusion), calls=%async_computation.1 | async-start | bytes 5603328 | tf_op jit(solution)/shard_map/all_to_all | solution.py:42
  90.4 177.6 %all-gather.3.cloned.1.call-start = ((), (), s32[]{:S(2)}) async-start(), calls=%async_computation.3 | async-start | bytes 5242880 | tf_op jit(solution)/shard_map/all_gather | solution.py:57
  177.8 5.1 %copy-start.2 = (f32[512]{0:T(512)S(1)}, f32[512]{0:T(512)}, u32[]{:S(2)}) copy-start(f32[512]{0:T(512)} %param.12) | copy-start | bytes 6148
  188.0 1.8 copy-start.3
  189.7 159.2 %all-gather.5.cloned.1.call-start = ((), (), s32[]{:S(2)}) async-start(), calls=%async_computation.4 | async-start | bytes 5242880 | tf_op jit(solution)/shard_map/all_gather | solution.py:58
  274.3 27.4 %copy-start.1 = (pred[2,512,2048]{2,1,0:T(8,128)(4,1)S(1)}, pred[2,512,2048]{2,1,0:T(8,128)(4,1)}, u32[]{:S(2)}) copy-start(pred[2,512,2048]{2,1,0:T(8,128)(4,1)} %broadcast_and_fusion) | copy-start | bytes 6291460
  382.1 3.0 copy-start.4
  382.2 3.0 copy-start.5
Sparse Core Ops, SparseCore 0:
  189.8 78.1 all-gather.2
  269.6 79.2 all-gather.4
where the time goes:
time: 415 us; the launch traced here: 410 us
  waiting for transfers between devices  131 us (32%)
  local copies, waits for them, and re-layouts  90.2 us (22%)
  matrix products  77.2 us (19%)
  blocking collectives  49.5 us (12%)
  other arithmetic  42.8 us (10%)
  between operations  13.7 us (3%)
  starting transfers between devices  5.8 us (1%)
    all_gather x1, waiting for transfers between devices, local(): key_piece = lax.all_gather(keys, 'cols', axis=1, tiled=True)  73.6 us
    all_to_all x1, waiting for transfers between devices, local(): lax.all_to_all(looked, 'rows', split_axis=0, concat_axis=0, tiled=True)  32.8 us
    all_to_all x1, blocking collectives, local(): lax.all_to_all(embedded, 'cols', split_axis=1, concat_axis=2, tiled=True)  28.5 us
    gather x2, local copies, waits for them, and re-layouts, local(): looked = jnp.take(table, jnp.maximum(asked, 0), axis=0)  27.9 us
    dot_general x1, matrix products, local(): jnp.einsum('bqhd,bkhd->bhqk', queries, key_heads, preferred_element_type=...  27.4 us
    dot_general x1, matrix products, local(): jnp.einsum('bhqk,bkhd->bhqd', probs.astype(jnp.bfloat16), value_heads, pr...  27 us
    all_gather x1, waiting for transfers between devices, local(): value_piece = lax.all_gather(values, 'cols', axis=1, tiled=True)  24.8 us
    reduce_sum x1, other arithmetic, local(): running_sum = jnp.sum(probs, axis=-1)  22.4 us
  transfers between devices with their start and end apart: 3, of which 3 were waited for; matrix products, arithmetic and copies ran while one was open for 15% of the time, Pallas kernels for 0%

commit v1 on v0

v1 whole, which is shorter than its diff:
```python
import functools

import jax
import jax.numpy as jnp
from jax import lax
from jax.experimental import pallas as pl
from jax.experimental.pallas import tpu as pltpu
from jax.sharding import PartitionSpec as P

HEADS = 8
LANES = 128
NEG = -1e30
SCORE_SCALE = 0.125 * 1.4426950408889634
MESH = pl.DeviceIdType.MESH
BF = jnp.bfloat16
F32 = jnp.float32


def rms_norm(values_f32, gain):
    mean_sq = jnp.mean(values_f32 * values_f32, axis=-1, keepdims=True)
    return values_f32 * lax.rsqrt(mean_sq + 1e-06) * gain


def layer_kernel(
    cols, lens_ref, e_ref, gain1, gain2, wq_h, wk_h, wv_h, wo_h, wi_h, wd_h, out_ref,
    ebuf, wq, wk, wv, wo, wi, wd, qm, k_s, v_s, m_s, l_s, acc,
    send_sem, recv_sem, own_sem, w_sem,
):
    me = lax.axis_index("cols")
    batch, full, width = e_ref.shape
    quarter = full // cols
    head_dim = LANES // 2

    def chunk(j):
        return pl.ds(pl.multiple_of(j * quarter, quarter), quarter)

    def slice_copy(b, source, target, j):
        return pltpu.make_async_remote_copy(
            src_ref=e_ref.at[b, chunk(j)],
            dst_ref=ebuf.at[source, b, chunk(j)],
            send_sem=send_sem.at[b, target, j],
            recv_sem=recv_sem.at[b, source, j],
            device_id={"cols": target},
            device_id_type=MESH,
        )

    barrier = pltpu.get_barrier_semaphore()
    for off in range(1, cols):
        pl.semaphore_signal(
            barrier, inc=1, device_id={"cols": lax.rem(me + off, cols)}, device_id_type=MESH
        )
    pl.semaphore_wait(barrier, cols - 1)

    def for_sends(act):
        def step(i, carry):
            b, t = i // cols, lax.rem(i, cols)
            for d in reversed(range(cols)):
                j = jnp.where(t == 0, d, t - 1)

                @pl.when((me != d) & (t <= d))
                def _():
                    act(slice_copy(b, me, d, j))

            return carry

        lax.fori_loop(0, batch * cols, step, 0)

    for_sends(lambda copy: copy.start())
    own = pltpu.make_async_copy(e_ref, ebuf.at[me], own_sem)
    own.start()
    loads = [
        pltpu.make_async_copy(src, dst, w_sem.at[i])
        for i, (src, dst) in enumerate(
            ((wq_h, wq), (wk_h, wk), (wv_h, wv), (wo_h, wo), (wi_h, wi), (wd_h, wd))
        )
    ]
    for load in loads:
        load.start()
    own.wait()
    for load in loads:
        load.wait()

    dims_nt = (((1,), (1,)), ((), ()))

    def embedded(b, j):
        parts = [ebuf[s, b, chunk(j), :] for s in range(cols)]
        return jnp.concatenate(parts, axis=1).astype(F32)

    def history(b, carry):
        length = lens_ref[b]
        query_pos = me * quarter + lax.broadcasted_iota(jnp.int32, (1, quarter), 1)
        limit = jnp.minimum(query_pos + 1, length)

        def unit(t, carry):
            j = jnp.where(t == 0, me, t - 1)
            for s in range(cols):

                @pl.when(me != s)
                def _():
                    slice_copy(b, s, s, j).wait_recv()

            normed = rms_norm(embedded(b, j), gain1[...]).astype(BF)
            k_s[...] = jnp.dot(normed, wk[...], preferred_element_type=F32).astype(BF)
            v_s[...] = lax.dot_general(
                wv[...], normed, dims_nt, preferred_element_type=F32
            ).astype(BF)

            @pl.when(t == 0)
            def _():
                q_t = lax.dot_general(
                    wq[...], normed, dims_nt, preferred_element_type=F32
                ).astype(BF)
                zero = jnp.zeros((head_dim, quarter), BF)
                for h in range(HEADS):
                    mine = q_t[h * head_dim : (h + 1) * head_dim]
                    pair = (mine, zero) if h % 2 == 0 else (zero, mine)
                    qm[h] = jnp.concatenate(pair, axis=0)
                m_s[...] = jnp.full_like(m_s, NEG)
                l_s[...] = jnp.zeros_like(l_s)
                acc[...] = jnp.zeros_like(acc)

            key_pos = lax.broadcasted_iota(jnp.int32, (quarter, quarter), 0)
            keep = key_pos < limit - j * quarter

            def pair(p, carry):
                k_pair = k_s[:, pl.ds(pl.multiple_of(p * LANES, LANES), LANES)]
                for side in range(2):
                    h = 2 * p + side
                    s = jnp.dot(k_pair, qm[h], preferred_element_type=F32) * SCORE_SCALE
                    s = jnp.where(keep, s, NEG)
                    m_old = m_s[h]
                    m_new = jnp.maximum(m_old, jnp.max(s, axis=0, keepdims=True))
                    probs = jnp.exp2(s - m_new)
                    alpha = jnp.exp2(m_old - m_new)
                    m_s[h] = m_new
                    l_s[h] = l_s[h] * alpha + jnp.sum(probs, axis=0, keepdims=True)
                    v_t = v_s[pl.ds(pl.multiple_of(h * head_dim, head_dim), head_dim), :]
                    acc[h] = acc[h] * alpha + jnp.dot(
                        v_t, probs.astype(BF), preferred_element_type=F32
                    )
                return carry

            lax.fori_loop(0, HEADS // 2, pair, 0)
            return carry

        lax.fori_loop(0, me + 1, unit, 0)

        att_t = (acc[...] / l_s[...]).reshape(HEADS * head_dim, quarter)
        attended = att_t.T.astype(BF)
        hidden = (
            embedded(b, me) + jnp.dot(attended, wo[...], preferred_element_type=F32)
        ).astype(BF)
        hidden = hidden.astype(F32)
        normed_two = rms_norm(hidden, gain2[...]).astype(BF)
        ff = wd.shape[0]
        tile = 512
        total = hidden
        for f in range(0, ff, tile):
            gate = jnp.dot(normed_two, wi[:, f : f + tile], preferred_element_type=F32)
            up = jnp.dot(normed_two, wi[:, ff + f : ff + f + tile], preferred_element_type=F32)
            act = (gate / (1.0 + jnp.exp(-gate)) * up).astype(BF)
            total = total + jnp.dot(act, wd[f : f + tile, :], preferred_element_type=F32)
        out_ref[b] = total.astype(BF)
        return carry

    lax.fori_loop(0, batch, history, 0)
    for_sends(lambda copy: copy.wait_send())


def layer_call(cols, lengths, emb, gain1, gain2, w_qkv, w_out, w_in, w_down):
    batch, full, width = emb.shape
    quarter = full // cols
    d = width * cols
    wq_t = w_qkv[:, :d].T
    wk = w_qkv[:, d : 2 * d]
    wv_t = w_qkv[:, 2 * d :].T
    any_spec = pl.BlockSpec(memory_space=pl.ANY)
    vmem = pl.BlockSpec(memory_space=pltpu.VMEM)
    smem = pl.BlockSpec(memory_space=pltpu.SMEM)
    weights = (wq_t, wk, wv_t, w_out, w_in, w_down)
    head_dim = d // HEADS
    return pl.pallas_call(
        functools.partial(layer_kernel, cols),
        out_shape=jax.ShapeDtypeStruct((batch, quarter, d), BF),
        in_specs=[smem, any_spec, vmem, vmem] + [any_spec] * 6,
        out_specs=vmem,
        scratch_shapes=[pltpu.VMEM((cols, batch, full, width), BF)]
        + [pltpu.VMEM(w.shape, BF) for w in weights]
        + [
            pltpu.VMEM((HEADS, 2 * head_dim, quarter), BF),
            pltpu.VMEM((quarter, d), BF),
            pltpu.VMEM((d, quarter), BF),
            pltpu.VMEM((HEADS, 1, quarter), F32),
            pltpu.VMEM((HEADS, 1, quarter), F32),
            pltpu.VMEM((HEADS, head_dim, quarter), F32),
            pltpu.SemaphoreType.DMA((batch, cols, cols)),
            pltpu.SemaphoreType.DMA((batch, cols, cols)),
            pltpu.SemaphoreType.DMA,
            pltpu.SemaphoreType.DMA((6,)),
        ],
        compiler_params=pltpu.CompilerParams(
            collective_id=0, has_side_effects=True, vmem_limit_bytes=60 * 1024 * 1024
        ),
    )(lengths, emb, gain1.reshape(1, d), gain2.reshape(1, d), *weights)


def local(token_ids, lengths, table, attn_gain, w_qkv, w_out, mlp_gain, w_in, w_down):
    batch_dev, quarter = token_ids.shape
    col_count = lax.axis_size("cols")
    row_count = lax.axis_size("rows")
    full_len = quarter * col_count
    block_rows, col_width = table.shape
    own_ids = lax.all_gather(token_ids, "cols", axis=1, tiled=True)
    flat_ids = own_ids.reshape(-1)
    token_count = flat_ids.shape[0]
    capacity = -(-(8 * token_count // (3 * row_count)) // 16) * 16
    owner_block = flat_ids // block_rows
    offset = flat_ids - owner_block * block_rows
    onehot = (owner_block[:, None] == jnp.arange(row_count, dtype=jnp.int32)[None, :]).astype(
        jnp.int32
    )
    slot_rank = jnp.sum((jnp.cumsum(onehot, axis=0) - 1) * onehot, axis=1)
    slot_index = owner_block * capacity + slot_rank
    groups = -(-capacity // LANES)
    group_id = owner_block * groups + slot_rank // LANES
    left = (group_id[:, None] == jnp.arange(row_count * groups, dtype=jnp.int32)[None, :]).astype(BF)
    lane = slot_rank % LANES
    hit = lane[:, None] == jnp.arange(LANES, dtype=jnp.int32)[None, :]
    high = jnp.where(hit, (offset // LANES)[:, None], 0).astype(BF)
    low = jnp.where(hit, (offset % LANES)[:, None], 0).astype(BF)
    high = lax.dot_general(left, high, (((0,), (0,)), ((), ())), preferred_element_type=F32)
    low = lax.dot_general(left, low, (((0,), (0,)), ((), ())), preferred_element_type=F32)
    requests = (high * LANES + low).astype(jnp.int32)
    requests = requests.reshape(row_count, groups * LANES)[:, :capacity]
    asked = lax.all_to_all(requests, "rows", split_axis=0, concat_axis=0, tiled=True)
    looked = table.at[asked.reshape(-1)].get(mode="promise_in_bounds")
    returned = lax.all_to_all(looked, "rows", split_axis=0, concat_axis=0, tiled=True)
    emb = returned.at[slot_index].get(mode="promise_in_bounds")
    emb = emb.reshape(batch_dev, full_len, col_width)
    return layer_call(
        col_count, lengths, emb, attn_gain, mlp_gain, w_qkv, w_out, w_in, w_down
    )


def solution(mesh):
    in_specs = (P("rows", "cols"), P("rows"), P("rows", "cols"), P(), P(), P(), P(), P(), P())
    out_specs = P("rows", "cols", None)
    return jax.shard_map(local, mesh=mesh, in_specs=in_specs, out_specs=out_specs, check_vma=False)
```

time: 415 us -> 212 us (0.51); the launches traced: 410 us -> 212 us
  waiting for transfers between devices: 131 us -> 27.2 us
  Pallas kernels: 0 us -> 103 us
  matrix products: 77.2 us -> 4.84 us
  local copies, waits for them, and re-layouts: 90.2 us -> 47 us
  other arithmetic: 42.8 us -> 3.17 us
  blocking collectives: 49.5 us -> 20.8 us
  between operations: 13.7 us -> 0.13 us
    pallas_call x0 -> x1, Pallas kernels: none -> 103 us  [layer_call(): pl.pallas_call(functools.partial(layer_kernel, cols), out_shape=jax.Shape...]
    all_gather x2 -> x0, waiting for transfers between devices: 98.3 us -> none  [the longest x1 73.6 us: local(): key_piece = lax.all_gather(keys, 'cols', axis=1, tiled=True)]
    dot_general x6 -> x2, matrix products: 77.2 us -> 4.84 us  [the longest x1 2.42 us: local(): lax.dot_general(left, low, (((0,), (0,)), ((), ())), preferred_element_ty...]
    all_to_all x1 -> x0, blocking collectives: 28.5 us -> none  [local(): lax.all_to_all(embedded, 'cols', split_axis=1, concat_axis=2, tiled=True)]
    reduce_sum x3 -> x0, other arithmetic: 23 us -> none  [the longest x1 22.4 us: local(): running_sum = jnp.sum(probs, axis=-1)]
    scatter x1 -> x0, local copies, waits for them, and re-layouts: 15.5 us -> none  [local(): requests = requests.at[slot_index].set(flat_ids - owner_block * block_row...]
    reshape x2, local copies, waits for them, and re-layouts: 12.9 us -> 0.13 us  [the longest x1 0.12 us: local(): looked = table.at[asked.reshape(-1)].get(mode='promise_in_bounds')]
    all_gather x2 -> x0, local copies, waits for them, and re-layouts: 12.6 us -> none  [the longest x1 6.28 us: local(): key_piece = lax.all_gather(keys, 'cols', axis=1, tiled=True)]
  transfers between devices with their start and end apart: 3 -> 1, of which waited for: 3 -> 1; matrix products, arithmetic and copies ran while one was open for 15% -> 3% of each run, Pallas kernels for 0% -> 0%
where the time goes in v1:
time: 212 us
  Pallas kernels  103 us (49%)
  local copies, waits for them, and re-layouts  47 us (22%)
  waiting for transfers between devices  27.2 us (13%)
  blocking collectives  20.8 us (10%)
  starting transfers between devices  5.01 us (2%)
  matrix products  4.84 us (2%)
  other arithmetic  3.17 us (1%)
    pallas_call x1, Pallas kernels, layer_call(): pl.pallas_call(functools.partial(layer_kernel, cols), out_shape=jax.Shape...  103 us
    all_to_all x1, waiting for transfers between devices, local(): lax.all_to_all(looked, 'rows', split_axis=0, concat_axis=0, tiled=True)  27.2 us
    gather x1, local copies, waits for them, and re-layouts, local(): looked = table.at[asked.reshape(-1)].get(mode='promise_in_bounds')  23.7 us
    gather x1, local copies, waits for them, and re-layouts, local(): emb = returned.at[slot_index].get(mode='promise_in_bounds')  15 us
    all_gather x1, blocking collectives, local(): own_ids = lax.all_gather(token_ids, 'cols', axis=1, tiled=True)  13.3 us
    all_to_all x1, blocking collectives, local(): lax.all_to_all(requests, 'rows', split_axis=0, concat_axis=0, tiled=True)  7.5 us
    unnamed x5, local copies, waits for them, and re-layouts  5.36 us
    all_to_all x1, starting transfers between devices, local(): lax.all_to_all(looked, 'rows', split_axis=0, concat_axis=0, tiled=True)  5.01 us
  transfers between devices with their start and end apart: 1, of which 1 were waited for; matrix products, arithmetic and copies ran while one was open for 3% of the time, Pallas kernels for 0%

profile of v1, /device:TPU:26, one launch (start us, length us, event | category | flops | bytes accessed | tf_op | source)
XLA Modules:
  0.0 211.5 jit_solution(7588195970719247408)
XLA Ops:
  0.0 13.3 %all_gather.3 = s32[2,2048]{1,0:T(2,128)S(1)} all-gather(s32[2,512]{1,0:T(2,128)} %param.9), channel_id=1, replica_groups=mesh['rows'=8,'cols'=4] {'cols'}, dimensions={1}, use_global_device_ids=true | all-gather | bytes 20480 | tf_op jit(solution)/shard_map/all_gather | solution.py:213
  13.4 2.3 %reduce-window.6 = s32[8,32,128]{2,1,0:T(8,128)S(1)} reduce-window(s32[8,32,128]{2,1,0:T(8,128)S(1)} %fusion.15, s32[]{:T(128)} %constant.59.clone.1), window={size=1x1x128 pad=0_0x0_0x127_0}, to_apply=%region_0.1 | reduce-window | flops 4161536 | bytes 262148 | tf_op jit(solution)/shard_map/reduce-window
  15.7 0.3 slice_reduce_fusion
  16.0 0.2 reduce-window.9
  16.2 0.1 add_bitcast_fusion
  16.4 0.1 fusion.14
  16.5 2.4 %fusion.2 = f32[88,128]{1,0:T(8,128)S(1)} fusion(s32[4096]{0:T(1024)S(1)} %get-tuple-element.11, s32[4096]{0:T(1024)S(1)} %get-tuple-element.10, s32[4096]{0:T(1024)S(1)} %get-tuple-element.9), kind=kOutput, calls=%fused_computation.8 | convolution fusion | flops 94219264 | bytes 94208 | tf_op jit(solution)/shard_map/dot_general | solution.py:231
  19.0 2.4 %fusion.4 = s32[88,128]{1,0:T(8,128)S(1)} fusion(f32[88,128]{1,0:T(8,128)S(1)} %fusion.2, s32[4096]{0:T(1024)S(1)} %get-tuple-element.8, s32[4096]{0:T(1024)S(1)} %get-tuple-element.10, s32[4096]{0:T(1024)S(1)} %get-tuple-element.9), kind=kOutput, calls=%fused_computation.10 | convolution fusion | flops 94230528 | bytes 139264 | tf_op jit(solution)/shard_map/dot_general | solution.py:232
  21.4 7.5 %all_to_all.21 = s32[8,1,1376]{2,1,0:T(1,128)S(1)} all-to-all(s32[8,1,1376]{2,1,0:T(1,128)S(1)} %all_to_all.14), channel_id=1, replica_groups=mesh['rows'=8,'cols'=4] {'rows'}, dimensions={0} | all-to-all | bytes 88064 | tf_op jit(solution)/shard_map/all_to_all | solution.py:235
  28.9 0.1 reduce.1
  29.0 0.1 reshape.271
  29.2 0.1 fusion.16
  29.3 23.7 %gather_fusion = bf16[11008,128]{1,0:T(8,128)(2,1)} fusion(bf16[16384,128]{1,0:T(8,128)(2,1)} %param.11, s32[11264]{0:T(1024)S(1)} %pad_clamp_fusion), kind=kCustom, calls=%fused_computation | custom fusion | bytes 5680128 | tf_op jit(solution)/shard_map/gather | solution.py:236
  53.0 5.0 %all-to-all-start.1 = ((bf16[8,1376,128]{2,1,0:T(8,128)(2,1)}), bf16[8,1376,128]{2,1,0:T(8,128)(2,1)S(1)}, u32[]{:S(2)}, u32[]{:S(2)}) async-start(bf16[8,1376,128]{2,1,0:T(8,128)(2,1)} %bitcast.32), calls=%async_computation.1 | async-start | bytes 5636096 | tf_op jit(solution)/shard_map/all_to_all | solution.py:237
  58.1 2.4 %fusion.28 = (bf16[512,512]{1,0:T(8,128)(2,1)S(1)}, bf16[512,512]{1,0:T(8,128)(2,1)}, bf16[512,512]{1,0:T(8,128)(2,1)}) fusion(bf16[512,1536]{1,0:T(8,128)(2,1)} %param.13), kind=kLoop, calls=%fused_computation.70 | loop fusion | bytes 3145728 | tf_op jit(solution)/shard_map/slice | solution.py:176
  60.5 2.1 copy.16
  62.6 1.0 copy.17
  63.6 0.1 compare_select_fusion.1
  63.7 27.2 %all-to-all-done.1 = bf16[8,1376,128]{2,1,0:T(8,128)(2,1)S(1)} async-done(((bf16[8,1376,128]{2,1,0:T(8,128)(2,1)}), bf16[8,1376,128]{2,1,0:T(8,128)(2,1)S(1)}, u32[]{:S(2)}, u32[]{:S(2)}) %all-to-all-start.1) | async-done | bytes 2818080 | tf_op jit(solution)/shard_map/all_to_all | solution.py:237
  90.9 15.0 %gather_fusion.1 = bf16[4096,128]{1,0:T(8,128)(2,1)} fusion(bf16[11008,128]{1,0:T(8,128)(2,1)S(1)} %bitcast.31, s32[4096]{0:T(1024)S(1)} %broadcast_clamp_fusion), kind=kCustom, calls=%fused_computation.1 | custom fusion | bytes 2113536 | tf_op jit(solution)/shard_map/gather | solution.py:238
  105.9 103.3 %shard_map.91 = bf16[2,512,512]{2,1,0:T(8,128)(2,1)} custom-call(s32[2]{0:T(128)} %lens_ref.1, bf16[2,2048,128]{2,1,0:T(8,128)(2,1)} %bitcast.33, f32[1,512]{1,0:T(1,128)} %bitcast.45, f32[1,512]{1,0:T(1,128)} %bitcast.46, bf16[512,512]{1,0:T(8,128)(2,1)} %bitcast.34, bf16[512,512]{1,0:T(8,128)(2,1)} %get-tuple-element.7.wk_h, bf16[512,512]{1,0:T(8,128)(2,1)} %bitcast.35, ...), custom_call_target="tpu_custom_call" | custom-call | tf_op jit(solution)/shard_map/pallas_call | solution.py:182
  209.3 2.3 %copy.23 = bf16[2,512,512]{2,1,0:T(8,128)(2,1)} copy(bf16[2,512,512]{2,1,0:T(8,128)(2,1)} %shard_map.91) | data formatting | bytes 2097152
  (11 shorter events, 0.2 us)
Async XLA Ops:
  53.0 37.9 %all-to-all-start.1 = ((bf16[8,1376,128]{2,1,0:T(8,128)(2,1)}), bf16[8,1376,128]{2,1,0:T(8,128)(2,1)S(1)}, u32[]{:S(2)}, u32[]{:S(2)}) async-start(bf16[8,1376,128]{2,1,0:T(8,128)(2,1)} %bitcast.32), calls=%async_computation.1 | async-start | bytes 5636096 | tf_op jit(solution)/shard_map/all_to_all | solution.py:237

commit v2 on v1

--- a/solution.py
+++ b/solution.py
@@ -24,7 +24,7 @@
 def layer_kernel(
     cols, lens_ref, e_ref, gain1, gain2, wq_h, wk_h, wv_h, wo_h, wi_h, wd_h, out_ref,
     ebuf, wq, wk, wv, wo, wi, wd, qm, k_s, v_s, m_s, l_s, acc,
-    send_sem, recv_sem, own_sem, w_sem,
+    send_sem, recv_sem, relay_sem, own_sem, w_sem,
 ):
     me = lax.axis_index("cols")
     batch, full, width = e_ref.shape
@@ -44,6 +44,19 @@
             device_id_type=MESH,
         )
 
+    def relay_copy(b, source, j):
+        return pltpu.make_async_remote_copy(
+            src_ref=ebuf.at[source, b, chunk(j)],
+            dst_ref=ebuf.at[source, b, chunk(j)],
+            send_sem=relay_sem.at[b, source, j],
+            recv_sem=recv_sem.at[b, source, j],
+            device_id={"cols": lax.rem(me + 1, cols)},
+            device_id_type=MESH,
+        )
+
+    def relays(source):
+        return (me + 1 < cols) & (me + 1 - source >= 3)
+
     barrier = pltpu.get_barrier_semaphore()
     for off in range(1, cols):
         pl.semaphore_signal(
@@ -57,7 +70,7 @@
             for d in reversed(range(cols)):
                 j = jnp.where(t == 0, d, t - 1)
 
-                @pl.when((me != d) & (t <= d))
+                @pl.when((me != d) & (t <= d) & ((d - me < 3) | (t == 0)))
                 def _():
                     act(slice_copy(b, me, d, j))
 
@@ -77,7 +90,7 @@
     for load in loads:
         load.start()
     own.wait()
-    for load in loads:
+    for load in loads[:3]:
         load.wait()
 
     dims_nt = (((1,), (1,)), ((), ()))
@@ -98,6 +111,12 @@
                 @pl.when(me != s)
                 def _():
                     slice_copy(b, s, s, j).wait_recv()
+
+            for s in range(cols - 3):
+
+                @pl.when(relays(s))
+                def _():
+                    relay_copy(b, s, j).start()
 
             normed = rms_norm(embedded(b, j), gain1[...]).astype(BF)
             k_s[...] = jnp.dot(normed, wk[...], preferred_element_type=F32).astype(BF)
@@ -145,6 +164,11 @@
 
         lax.fori_loop(0, me + 1, unit, 0)
 
+        @pl.when(b == 0)
+        def _():
+            for load in loads[3:]:
+                load.wait()
+
         att_t = (acc[...] / l_s[...]).reshape(HEADS * head_dim, quarter)
         attended = att_t.T.astype(BF)
         hidden = (
@@ -165,6 +189,17 @@
 
     lax.fori_loop(0, batch, history, 0)
     for_sends(lambda copy: copy.wait_send())
+
+    def relay_ends(i, carry):
+        for s in range(cols - 3):
+
+            @pl.when(relays(s) & (lax.rem(i, cols) <= me))
+            def _():
+                relay_copy(i // cols, s, lax.rem(i, cols)).wait_send()
+
+        return carry
+
+    lax.fori_loop(0, batch * cols, relay_ends, 0)
 
 
 def layer_call(cols, lengths, emb, gain1, gain2, w_qkv, w_out, w_in, w_down):
@@ -193,6 +228,7 @@
             pltpu.VMEM((HEADS, 1, quarter), F32),
             pltpu.VMEM((HEADS, 1, quarter), F32),
             pltpu.VMEM((HEADS, head_dim, quarter), F32),
+            pltpu.SemaphoreType.DMA((batch, cols, cols)),
             pltpu.SemaphoreType.DMA((batch, cols, cols)),
             pltpu.SemaphoreType.DMA((batch, cols, cols)),
             pltpu.SemaphoreType.DMA,

time: 212 us -> 212 us (level)
  no operation moved by 1% of the time
where the time goes in v2:
time: 212 us
  Pallas kernels  103 us (49%)
  local copies, waits for them, and re-layouts  47 us (22%)
  waiting for transfers between devices  27.2 us (13%)
  blocking collectives  20.8 us (10%)
  starting transfers between devices  5.01 us (2%)
  matrix products  4.84 us (2%)
  other arithmetic  3.17 us (1%)
    pallas_call x1, Pallas kernels, layer_call(): pl.pallas_call(functools.partial(layer_kernel, cols), out_shape=jax.Shape...  103 us
    all_to_all x1, waiting for transfers between devices, local(): lax.all_to_all(looked, 'rows', split_axis=0, concat_axis=0, tiled=True)  27.2 us
    gather x1, local copies, waits for them, and re-layouts, local(): looked = table.at[asked.reshape(-1)].get(mode='promise_in_bounds')  23.7 us
    gather x1, local copies, waits for them, and re-layouts, local(): emb = returned.at[slot_index].get(mode='promise_in_bounds')  15 us
    all_gather x1, blocking collectives, local(): own_ids = lax.all_gather(token_ids, 'cols', axis=1, tiled=True)  13.3 us
    all_to_all x1, blocking collectives, local(): lax.all_to_all(requests, 'rows', split_axis=0, concat_axis=0, tiled=True)  7.5 us
    unnamed x5, local copies, waits for them, and re-layouts  5.36 us
    all_to_all x1, starting transfers between devices, local(): lax.all_to_all(looked, 'rows', split_axis=0, concat_axis=0, tiled=True)  5.01 us
  transfers between devices with their start and end apart: 1, of which 1 were waited for; matrix products, arithmetic and copies ran while one was open for 3% of the time, Pallas kernels for 0%

profile of v2, /device:TPU:26, one launch (start us, length us, event | category | flops | bytes accessed | tf_op | source)
XLA Modules:
  0.0 211.6 jit_solution(2483373440694197140)
XLA Ops:
  0.0 13.3 %all_gather.3 = s32[2,2048]{1,0:T(2,128)S(1)} all-gather(s32[2,512]{1,0:T(2,128)} %param.9), channel_id=1, replica_groups=mesh['rows'=8,'cols'=4] {'cols'}, dimensions={1}, use_global_device_ids=true | all-gather | bytes 20480 | tf_op jit(solution)/shard_map/all_gather | solution.py:249
  13.4 2.3 %reduce-window.6 = s32[8,32,128]{2,1,0:T(8,128)S(1)} reduce-window(s32[8,32,128]{2,1,0:T(8,128)S(1)} %fusion.15, s32[]{:T(128)} %constant.59.clone.1), window={size=1x1x128 pad=0_0x0_0x127_0}, to_apply=%region_0.1 | reduce-window | flops 4161536 | bytes 262148 | tf_op jit(solution)/shard_map/reduce-window
  15.7 0.3 slice_reduce_fusion
  16.0 0.2 reduce-window.9
  16.2 0.1 add_bitcast_fusion
  16.4 0.1 fusion.14
  16.5 2.4 %fusion.2 = f32[88,128]{1,0:T(8,128)S(1)} fusion(s32[4096]{0:T(1024)S(1)} %get-tuple-element.11, s32[4096]{0:T(1024)S(1)} %get-tuple-element.10, s32[4096]{0:T(1024)S(1)} %get-tuple-element.9), kind=kOutput, calls=%fused_computation.8 | convolution fusion | flops 94219264 | bytes 94208 | tf_op jit(solution)/shard_map/dot_general | solution.py:267
  19.0 2.4 %fusion.4 = s32[88,128]{1,0:T(8,128)S(1)} fusion(f32[88,128]{1,0:T(8,128)S(1)} %fusion.2, s32[4096]{0:T(1024)S(1)} %get-tuple-element.8, s32[4096]{0:T(1024)S(1)} %get-tuple-element.10, s32[4096]{0:T(1024)S(1)} %get-tuple-element.9), kind=kOutput, calls=%fused_computation.10 | convolution fusion | flops 94230528 | bytes 139264 | tf_op jit(solution)/shard_map/dot_general | solution.py:268
  21.4 7.5 %all_to_all.21 = s32[8,1,1376]{2,1,0:T(1,128)S(1)} all-to-all(s32[8,1,1376]{2,1,0:T(1,128)S(1)} %all_to_all.14), channel_id=1, replica_groups=mesh['rows'=8,'cols'=4] {'rows'}, dimensions={0} | all-to-all | bytes 88064 | tf_op jit(solution)/shard_map/all_to_all | solution.py:271
  28.9 0.1 reduce.1
  29.0 0.1 reshape.271
  29.2 0.1 fusion.16
  29.3 23.7 %gather_fusion = bf16[11008,128]{1,0:T(8,128)(2,1)} fusion(bf16[16384,128]{1,0:T(8,128)(2,1)} %param.11, s32[11264]{0:T(1024)S(1)} %pad_clamp_fusion), kind=kCustom, calls=%fused_computation | custom fusion | bytes 5680128 | tf_op jit(solution)/shard_map/gather | solution.py:272
  53.0 5.0 %all-to-all-start.1 = ((bf16[8,1376,128]{2,1,0:T(8,128)(2,1)}), bf16[8,1376,128]{2,1,0:T(8,128)(2,1)S(1)}, u32[]{:S(2)}, u32[]{:S(2)}) async-start(bf16[8,1376,128]{2,1,0:T(8,128)(2,1)} %bitcast.32), calls=%async_computation.1 | async-start | bytes 5636096 | tf_op jit(solution)/shard_map/all_to_all | solution.py:273
  58.1 2.4 %fusion.28 = (bf16[512,512]{1,0:T(8,128)(2,1)S(1)}, bf16[512,512]{1,0:T(8,128)(2,1)}, bf16[512,512]{1,0:T(8,128)(2,1)}) fusion(bf16[512,1536]{1,0:T(8,128)(2,1)} %param.13), kind=kLoop, calls=%fused_computation.70 | loop fusion | bytes 3145728 | tf_op jit(solution)/shard_map/slice | solution.py:211
  60.5 2.1 copy.16
  62.6 1.0 copy.17
  63.6 0.1 compare_select_fusion.1
  63.7 27.2 %all-to-all-done.1 = bf16[8,1376,128]{2,1,0:T(8,128)(2,1)S(1)} async-done(((bf16[8,1376,128]{2,1,0:T(8,128)(2,1)}), bf16[8,1376,128]{2,1,0:T(8,128)(2,1)S(1)}, u32[]{:S(2)}, u32[]{:S(2)}) %all-to-all-start.1) | async-done | bytes 2818080 | tf_op jit(solution)/shard_map/all_to_all | solution.py:273
  90.9 15.0 %gather_fusion.1 = bf16[4096,128]{1,0:T(8,128)(2,1)} fusion(bf16[11008,128]{1,0:T(8,128)(2,1)S(1)} %bitcast.31, s32[4096]{0:T(1024)S(1)} %broadcast_clamp_fusion), kind=kCustom, calls=%fused_computation.1 | custom fusion | bytes 2113536 | tf_op jit(solution)/shard_map/gather | solution.py:274
  105.9 103.4 %shard_map.91 = bf16[2,512,512]{2,1,0:T(8,128)(2,1)} custom-call(s32[2]{0:T(128)} %lens_ref.1, bf16[2,2048,128]{2,1,0:T(8,128)(2,1)} %bitcast.33, f32[1,512]{1,0:T(1,128)} %bitcast.45, f32[1,512]{1,0:T(1,128)} %bitcast.46, bf16[512,512]{1,0:T(8,128)(2,1)} %bitcast.34, bf16[512,512]{1,0:T(8,128)(2,1)} %get-tuple-element.7.wk_h, bf16[512,512]{1,0:T(8,128)(2,1)} %bitcast.35, ...), custom_call_target="tpu_custom_call" | custom-call | tf_op jit(solution)/shard_map/pallas_call | solution.py:217
  209.4 2.3 %copy.23 = bf16[2,512,512]{2,1,0:T(8,128)(2,1)} copy(bf16[2,512,512]{2,1,0:T(8,128)(2,1)} %shard_map.91) | data formatting | bytes 2097152
  (11 shorter events, 0.2 us)
Async XLA Ops:
  53.0 37.9 %all-to-all-start.1 = ((bf16[8,1376,128]{2,1,0:T(8,128)(2,1)}), bf16[8,1376,128]{2,1,0:T(8,128)(2,1)S(1)}, u32[]{:S(2)}, u32[]{:S(2)}) async-start(bf16[8,1376,128]{2,1,0:T(8,128)(2,1)} %bitcast.32), calls=%async_computation.1 | async-start | bytes 5636096 | tf_op jit(solution)/shard_map/all_to_all | solution.py:273
